TPU v7x, 32 devices: a whole 2x2x4 slice. The times are simulated.
32 devices in a mesh: groups: 2 (over y), blk: 4 (over z), heads: 2 (over x), beam: 2 (over core).
Axes of the slice: x: 2, y: 2, z: 4, core: 2. Of those that a mesh axis runs over, the one named last changes fastest.
Arguments:
- queries: bfloat16 [4, 32, 64, 128], P(('groups', 'beam'), 'blk', 'heads'), parts along dimension 0, may hold values from -110 to 110
- positions: int32 [4, 32], P(('groups', 'beam'), 'blk'), parts along dimension 0, may hold values from 512 to 4096
- row_order: int32 [4, 32], P(('groups', 'beam')), parts along dimension 0, may hold values from 0 to 31, each once within a row
- lengths: int32 [8], P(('groups', 'blk')), parts along dimension 0, may hold values from 128 to 1024
- cache_keys: bfloat16 [8, 4, 1024, 128], P(('groups', 'blk'), 'heads'), parts along dimension 0, may hold values from -4 to 4
- cache_values: bfloat16 [8, 4, 1024, 128], P(('groups', 'blk'), 'heads'), parts along dimension 0, may hold values from -6 to 6
Outputs:
- attended: bfloat16 [4, 32, 64, 128], P(('groups', 'beam'), 'blk', 'heads'), parts along dimension 0
There are 2 independent parts, one for each index of `groups`. A program takes and returns all parts, laid end to end along the dimension named above; each array names one. Nothing has to cross between parts.
Inputs may be any that keep to these rules, and one draw needn't show every extreme that they name: Slots of shard s from lengths[s] on hold no cache entry. row_order[e] is a permutation of 0 to 31.
All inputs are finite; a program needn't handle non-finite values.
Results may differ from a plain program's by a relative error of at most 0.0015.
Values may be sent and summed in bfloat16 or wider, within the bound.
A program may use at most 64 MiB of HBM per device.

v0:
```python
import jax
import jax.numpy as jnp
from jax import lax
from jax.sharding import PartitionSpec as P

KB = 256


masked_score = -1e30


def entering(value, axis, join, neutral):
    count, mine = (lax.axis_size(axis), lax.axis_index(axis))
    pieces = lax.all_gather(value, axis)
    total = jnp.full_like(value, 0) + jnp.asarray(neutral, value.dtype)

    def turn(position, total):
        longer = join(total, pieces[position])
        return jnp.where(position < mine, longer, total)

    return lax.fori_loop(0, count - 1, turn, total)


def add_counts(earlier, later):
    return earlier + later


def block_partial(
    query_rows, row_positions, key_block, value_block, first_slot, length, offset, scaling
):
    scores = (
        jnp.einsum("rkgd,kjd->rkgj", query_rows, key_block, preferred_element_type=jnp.float32)
        * scaling
    )
    slot_ids = first_slot + lax.iota(jnp.int32, key_block.shape[1])
    visible = (slot_ids < length)[None, :] & ((offset + slot_ids)[None, :] < row_positions[:, None])
    visible = visible[:, None, None, :]
    highest = jnp.max(jnp.where(visible, scores, masked_score), axis=-1)
    weights = jnp.where(visible, jnp.exp(scores - highest[..., None]), 0.0)
    totals = jnp.sum(weights, axis=-1)
    block_out = jnp.einsum(
        "rkgj,kjd->rkgd",
        weights.astype(jnp.bfloat16),
        value_block,
        preferred_element_type=jnp.float32,
    )
    return (block_out, totals, highest)


def combine_parts(running, latest):
    run_out, run_tot, run_top = running
    new_out, new_tot, new_top = latest
    joined = jnp.maximum(run_top, new_top)
    older = jnp.exp(run_top - joined)
    newer = jnp.exp(new_top - joined)
    return (
        run_out * older[..., None] + new_out * newer[..., None],
        run_tot * older + new_tot * newer,
        joined,
    )


def settle(exchanged):
    shard_out, shard_tot, shard_top = exchanged
    highest = jnp.max(shard_top, axis=0)
    factor = jnp.exp(shard_top - highest)
    numerator = jnp.sum(shard_out * factor[..., None], axis=0)
    denominator = jnp.sum(shard_tot * factor, axis=0)
    return numerator / denominator[..., None]


def per_device(queries, positions, row_order, lengths, cache_keys, cache_values):
    offsets = entering(lengths, "blk", add_counts, jnp.zeros_like(lengths))
    length = lengths[0]
    offset = offsets[0]
    key_shard = cache_keys[0]
    value_shard = cache_values[0]
    kv_heads = key_shard.shape[0]
    capacity = key_shard.shape[1]
    head_dim = key_shard.shape[2]
    group = queries.shape[2] // kv_heads
    scaling = float(head_dim) ** (-0.5)
    row_dev = queries.shape[1]
    piece_queries = lax.all_gather(queries, "blk", axis=1, tiled=True)
    piece_positions = lax.all_gather(positions, "blk", axis=1, tiled=True)
    count_rows = piece_queries.shape[1]
    query_rows = piece_queries.reshape(count_rows, kv_heads, group, head_dim)
    row_positions = piece_positions.reshape(count_rows)
    shard_count_rows = query_rows.shape[0]
    running = (
        jnp.zeros((shard_count_rows, kv_heads, group, head_dim), jnp.float32),
        jnp.zeros((shard_count_rows, kv_heads, group), jnp.float32),
        jnp.full((shard_count_rows, kv_heads, group), masked_score, jnp.float32),
    )
    for block in range(capacity // KB):
        first_slot = block * KB
        latest = block_partial(
            query_rows,
            row_positions,
            key_shard[:, first_slot : first_slot + KB],
            value_shard[:, first_slot : first_slot + KB],
            first_slot,
            length,
            offset,
            scaling,
        )
        running = combine_parts(running, latest)
    merged_out, merged_tot, merged_top = tuple((fresh for fresh in running))
    picked = row_order[0]
    merged_out = jnp.take(merged_out, picked, axis=0)
    merged_tot = jnp.take(merged_tot, picked, axis=0)
    merged_top = jnp.take(merged_top, picked, axis=0)
    result = settle(
        (
            lax.all_to_all(merged_out[None], "blk", split_axis=1, concat_axis=0, tiled=True),
            lax.all_to_all(merged_tot[None], "blk", split_axis=1, concat_axis=0, tiled=True),
            lax.all_to_all(merged_top[None], "blk", split_axis=1, concat_axis=0, tiled=True),
        )
    )
    return result.reshape(1, row_dev, kv_heads * group, head_dim).astype(jnp.bfloat16)


def solution(mesh):
    placed = (
        P(("groups", "beam"), "blk", "heads", None),
        P(("groups", "beam"), "blk"),
        P(("groups", "beam"), None),
        P(("groups", "blk")),
        P(("groups", "blk"), "heads", None, None),
        P(("groups", "blk"), "heads", None, None),
    )
    return jax.shard_map(
        per_device,
        mesh=mesh,
        in_specs=placed,
        out_specs=P(("groups", "beam"), "blk", "heads", None),
        check_vma=False,
    )
```

profile of v0, /device:TPU:0, one launch (start us, length us, event | category | flops | bytes accessed | tf_op | source)
XLA Modules:
  0.0 70.3 jit_solution(5707162377590074350)
XLA Ops:
  0.7 0.6 copy-done.5
  1.3 0.6 dynamic-slice
  2.5 0.7 dynamic-update-slice
  3.1 0.7 copy-done.3
  3.9 9.9 %all-reduce.2 = (s32[4]{0:T(128)S(1)}, s32[32]{0:T(128)S(1)}) all-reduce(s32[4]{0:T(128)S(1)} %dynamic-update-slice, s32[32]{0:T(128)S(1)} %bitcast_dynamic-update-slice_fusion), channel_id=2, replica_groups=mesh['groups'=2,'blk'=4,'heads'=2,'beam'=2] {'blk'}, use_global_device_ids=true, to_apply=%add | all-reduce | flops 36 | bytes 288
  13.8 3.7 %while.13 = (s32[]{:T(128)}, s32[1]{0:T(128)}, s32[]{:T(128)}, s32[4,1]{0,1:T(1,128)S(1)}, s32[]{:T(128)}) while((s32[]{:T(128)}, s32[1]{0:T(128)}, s32[]{:T(128)}, s32[4,1]{0,1:T(1,128)S(1)}, s32[]{:T(128)}) %tuple.58), condition=%wide.region_1.2_spmd, body=%wide.region_0.1_spmd.sunk | while | flops 5 | bytes 115 | solution.py:21
  13.8 0.6 constant_dynamic-slice_fusion.2
  15.1 0.6 constant_dynamic-slice_fusion.2
  16.3 0.6 constant_dynamic-slice_fusion.2
  17.7 13.8 %all_gather.15 = bf16[1,32,32,128]{3,2,0,1:T(8,128)(2,1)S(1)} all-gather(bf16[1,8,32,128]{3,2,0,1:T(8,128)(2,1)S(1)} %bitcast.162), channel_id=1, replica_groups=mesh['groups'=2,'blk'=4,'heads'=2,'beam'=2] {'blk'}, dimensions={1}, use_global_device_ids=true | all-gather | bytes 327680 | tf_op jit(solution)/shard_map/all_gather | solution.py:84
  33.2 0.4 fusion.20
  34.0 0.4 fusion.16
  35.1 0.6 gather_fusion.1
  35.7 0.6 gather_fusion.2
  36.4 0.7 %reshape.392 = f32[4,1,256]{2,1,0:T(1,128)} reshape(f32[32,1,2,16]{3,2,1,0:T(2,128)S(1)} %bitcast.161) | data formatting | bytes 8192
  37.1 3.6 %all-to-all-start.2 = ((f32[4,1,256]{2,1,0:T(1,128)}), f32[4,1,256]{2,1,0:T(1,128)S(1)}, u32[]{:S(2)}, u32[]{:S(2)}) async-start(f32[4,1,256]{2,1,0:T(1,128)} %reshape.392), calls=%async_computation.2 | async-start | bytes 8192 | tf_op jit(solution)/shard_map/all_to_all | solution.py:116
  41.2 0.5 fusion.14
  41.7 0.5 fusion.13
  42.2 0.5 fusion.12
  42.7 0.9 %fusion.11 = f32[32,2,16,128]{3,2,0,1:T(8,128)S(1)} fusion(f32[32,2,16,128]{3,2,0,1:T(8,128)S(1)} %fusion.14, f32[32,2,16,128]{3,2,0,1:T(8,128)S(1)} %fusion.13, f32[32,2,16,128]{3,2,0,1:T(8,128)S(1)} %fusion.12, bf16[32,2,16,256]{3,0,2,1:T(8,128)(2,1)S(1)} %get-tuple-element.106, f32[32,2,16]{2,0,1:T(8,128)S(1)} %copy.117, f32[32,2,16]{2,0,1:T(8,128)S(1)} %copy.114, ...), kind=kOutput, calls=%fused_computation.23 | convolution fusion | flops 68157440 | bytes 2916352 | tf_op jit(solution)/shard_map/rkgj,kjd->rkgd/dot_general | solution.py:41
  43.6 0.7 %reshape.390 = f32[4,1,256]{2,1,0:T(1,128)} reshape(f32[32,1,2,16]{3,2,1,0:T(2,128)S(1)} %bitcast.160) | data formatting | bytes 8192
  44.3 0.6 gather_fusion
  44.9 1.3 %all-to-all-done.2 = f32[4,1,256]{2,1,0:T(1,128)S(1)} async-done(((f32[4,1,256]{2,1,0:T(1,128)}), f32[4,1,256]{2,1,0:T(1,128)S(1)}, u32[]{:S(2)}, u32[]{:S(2)}) %all-to-all-start.2) | async-done | bytes 4128 | tf_op jit(solution)/shard_map/all_to_all | solution.py:116
  46.2 3.8 %all-to-all-start.1 = ((f32[4,1,256]{2,1,0:T(1,128)}), f32[4,1,256]{2,1,0:T(1,128)S(1)}, u32[]{:S(2)}, u32[]{:S(2)}) async-start(f32[4,1,256]{2,1,0:T(1,128)} %reshape.390), calls=%async_computation.1 | async-start | bytes 8192 | tf_op jit(solution)/shard_map/all_to_all | solution.py:117
  50.0 0.9 %fusion.23 = f32[1,32,2,16,128]{4,3,2,0,1:T(8,128)} fusion(f32[32,2,16,128]{3,2,1,0:T(8,128)S(1)} %gather_fusion, pred[32]{0:T(512)(128)(4,1)S(1)} %compare_and_fusion.4), kind=kLoop, calls=%fused_computation.44 | loop fusion | flops 131072 | bytes 1048608 | tf_op jit(solution)/shard_map/jit(_take)/select_n | solution.py:110
  50.9 4.7 %all-to-all-done.1 = f32[4,1,256]{2,1,0:T(1,128)S(1)} async-done(((f32[4,1,256]{2,1,0:T(1,128)}), f32[4,1,256]{2,1,0:T(1,128)S(1)}, u32[]{:S(2)}, u32[]{:S(2)}) %all-to-all-start.1) | async-done | bytes 4128 | tf_op jit(solution)/shard_map/all_to_all | solution.py:117
  55.6 3.5 %all-to-all-start = ((f32[1,32,2,16,128]{4,3,2,0,1:T(8,128)}), f32[1,32,2,16,128]{4,3,2,0,1:T(8,128)S(1)}, u32[]{:S(2)}, u32[]{:S(2)}) async-start(f32[1,32,2,16,128]{4,3,2,0,1:T(8,128)} %fusion.23), calls=%async_computation | async-start | bytes 1048576 | tf_op jit(solution)/shard_map/all_to_all | solution.py:115
  59.1 0.5 broadcast.265
  59.6 0.7 reduce
  60.4 0.7 reduce.1
  61.3 8.0 %all-to-all-done = f32[1,32,2,16,128]{4,3,2,0,1:T(8,128)S(1)} async-done(((f32[1,32,2,16,128]{4,3,2,0,1:T(8,128)}), f32[1,32,2,16,128]{4,3,2,0,1:T(8,128)S(1)}, u32[]{:S(2)}, u32[]{:S(2)}) %all-to-all-start) | async-done | bytes 524320 | tf_op jit(solution)/shard_map/all_to_all | solution.py:115
  69.5 0.7 %divide_convert_fusion = bf16[1,8,32,128]{3,2,1,0:T(8,128)(2,1)} fusion(f32[1,8,32,128]{3,2,1,0:T(8,128)S(1)} %bitcast.156, f32[8,32]{1,0:T(8,128)S(1)} %div.18), kind=kLoop, calls=%fused_computation.58 | loop fusion | flops 65536 | bytes 197632 | tf_op jit(solution)/shard_map/convert_element_type | solution.py:120
  (51 shorter events, 4.1 us)
Async XLA Ops:
  0.7 0.7 copy-start.5
  3.1 14.5 %copy-start.4 = (s32[1,32]{1,0:T(1,128)S(1)}, s32[1,32]{1,0:T(1,128)}, u32[]{:S(2)}) copy-start(s32[1,32]{1,0:T(1,128)} %param.12) | copy-start | bytes 388
  3.1 0.7 copy-start.3
  3.8 13.8 %copy-start.1 = (bf16[1,8,32,128]{3,2,1,0:T(8,128)(2,1)S(1)}, bf16[1,8,32,128]{3,2,1,0:T(8,128)(2,1)}, u32[]{:S(2)}) copy-start(bf16[1,8,32,128]{3,2,1,0:T(8,128)(2,1)} %param.10) | copy-start | bytes 196612
  13.8 17.8 %copy-start = (bf16[1,2,1024,128]{3,2,1,0:T(8,128)(2,1)S(1)}, bf16[1,2,1024,128]{3,2,1,0:T(8,128)(2,1)}, u32[]{:S(2)}) copy-start(bf16[1,2,1024,128]{3,2,1,0:T(8,128)(2,1)} %param.14) | copy-start | bytes 1572868
  34.8 6.4 %copy-start.2 = (bf16[1,2,1024,128]{3,2,1,0:T(8,128)(2,1)S(1)}, bf16[1,2,1024,128]{3,2,1,0:T(8,128)(2,1)}, u32[]{:S(2)}) copy-start(bf16[1,2,1024,128]{3,2,1,0:T(8,128)(2,1)} %param.15) | copy-start | bytes 1572868
  37.1 9.1 %all-to-all-start.2 = ((f32[4,1,256]{2,1,0:T(1,128)}), f32[4,1,256]{2,1,0:T(1,128)S(1)}, u32[]{:S(2)}, u32[]{:S(2)}) async-start(f32[4,1,256]{2,1,0:T(1,128)} %reshape.392), calls=%async_computation.2 | async-start | bytes 8192 | tf_op jit(solution)/shard_map/all_to_all | solution.py:116
  46.2 9.4 %all-to-all-start.1 = ((f32[4,1,256]{2,1,0:T(1,128)}), f32[4,1,256]{2,1,0:T(1,128)S(1)}, u32[]{:S(2)}, u32[]{:S(2)}) async-start(f32[4,1,256]{2,1,0:T(1,128)} %reshape.390), calls=%async_computation.1 | async-start | bytes 8192 | tf_op jit(solution)/shard_map/all_to_all | solution.py:117
  55.6 13.7 %all-to-all-start = ((f32[1,32,2,16,128]{4,3,2,0,1:T(8,128)}), f32[1,32,2,16,128]{4,3,2,0,1:T(8,128)S(1)}, u32[]{:S(2)}, u32[]{:S(2)}) async-start(f32[1,32,2,16,128]{4,3,2,0,1:T(8,128)} %fusion.23), calls=%async_computation | async-start | bytes 1048576 | tf_op jit(solution)/shard_map/all_to_all | solution.py:115
where the time goes:
time: 70.7 us; the launch traced here: 70.3 us
  blocking collectives  23.7 us (34%)
  waiting for transfers between devices  14 us (20%)
  starting transfers between devices  10.8 us (15%)
  local copies, waits for them, and re-layouts  9.41 us (13%)
  other arithmetic  5.07 us (7%)
  matrix products  3.86 us (5%)
  loops' own time  1.9 us (3%)
  between operations  1.49 us (2%)
    all_gather x1, blocking collectives, per_device(): piece_queries = lax.all_gather(queries, 'blk', axis=1, tiled=True)  13.8 us
    unnamed x1, blocking collectives  9.92 us
    all_to_all x1, waiting for transfers between devices, per_device(): lax.all_to_all(merged_out[None], 'blk', split_axis=1, concat_axis=0, tile...  8 us
    all_to_all x1, waiting for transfers between devices, per_device(): lax.all_to_all(merged_top[None], 'blk', split_axis=1, concat_axis=0, tile...  4.69 us
    unnamed x20, local copies, waits for them, and re-layouts  4.28 us
    all_to_all x1, starting transfers between devices, per_device(): lax.all_to_all(merged_top[None], 'blk', split_axis=1, concat_axis=0, tile...  3.78 us
    all_to_all x1, starting transfers between devices, per_device(): lax.all_to_all(merged_tot[None], 'blk', split_axis=1, concat_axis=0, tile...  3.56 us
    all_to_all x1, starting transfers between devices, per_device(): lax.all_to_all(merged_out[None], 'blk', split_axis=1, concat_axis=0, tile...  3.47 us
  transfers between devices with their start and end apart: 3, of which 3 were waited for; matrix products, arithmetic and copies ran while one was open for 10% of the time, Pallas kernels for 0%

commit v1 on v0

v1 whole, which is shorter than its diff:
```python
import functools
import math

import jax
import jax.numpy as jnp
from jax import lax
from jax.experimental import pallas as pl
from jax.experimental.pallas import tpu as pltpu
from jax.sharding import PartitionSpec as P

KB = 256
MASKED = -1e30
FLOOR = -1e29
MESH = pl.DeviceIdType.MESH


def flipped(place, mask, bits):
    total = 0
    for bit in range(bits):
        digit = lax.rem(lax.div(place, 1 << bit), 2)
        total = total + lax.rem(digit + ((mask >> bit) & 1), 2) * (1 << bit)
    return total


def kernel(
    n, scale,
    pos_ref, order_ref, len_ref, q_hbm, k_hbm, v_hbm,
    out_ref,
    meta, q_all, k_buf, v_buf, vt_buf, sent, came,
    local_sem, relay_send, relay_recv, part_send, part_recv,
):
    me = lax.axis_index("blk")
    rows, kv, group, width = q_hbm.shape
    cap = k_hbm.shape[1]
    lanes = rows * group
    bits = n.bit_length() - 1

    q_in = [
        pltpu.make_async_copy(
            q_hbm.at[:, h], q_all.at[h, pl.ds(me * rows, rows)], local_sem.at[2 * kv + h]
        )
        for h in range(kv)
    ]
    k_in = [pltpu.make_async_copy(k_hbm.at[h], k_buf.at[h], local_sem.at[h]) for h in range(kv)]
    v_in = [pltpu.make_async_copy(v_hbm.at[h], v_buf.at[h], local_sem.at[kv + h]) for h in range(kv)]
    for copy in q_in + k_in + v_in:
        copy.start()

    for r in range(rows):
        meta[me, pl.ds(r, 1), :] = jnp.full((1, 128), pos_ref[0, r], jnp.int32)
    meta[me, pl.ds(rows, 1), :] = jnp.full((1, 128), len_ref[0], jnp.int32)

    barrier = pltpu.get_barrier_semaphore()
    has = {1: me + 1 < n, -1: me >= 1}
    for k in range(1, n):
        pl.semaphore_signal(
            barrier, inc=1, device_id={"blk": flipped(me, k, bits)}, device_id_type=MESH
        )
    pl.semaphore_wait(barrier, n - 1)

    def slot(item, source):
        if item == 0:
            return meta.at[source]
        return q_all.at[item - 1, pl.ds(source * rows, rows)]

    def relay(item, step, hops):
        way = 0 if step == 1 else 1
        block = slot(item, me - step * hops)
        return pltpu.make_async_remote_copy(
            src_ref=block, dst_ref=block,
            send_sem=relay_send.at[item, way, hops],
            recv_sem=relay_recv.at[item, way, hops + 1],
            device_id={"blk": me + step}, device_id_type=MESH,
        )

    def arrival(item, step, hops):
        way = 0 if step == 1 else 1
        block = slot(item, me - step * hops)
        return pltpu.make_async_remote_copy(
            src_ref=block, dst_ref=block,
            send_sem=relay_send.at[item, way, hops],
            recv_sem=relay_recv.at[item, way, hops],
            device_id={"blk": me - step}, device_id_type=MESH,
        )

    def begin(item):
        for step in (1, -1):
            @pl.when(has[step])
            def _():
                relay(item, step, 0).start()

    def turn(item, hops):
        for step in (1, -1):
            source = me - step * hops
            there = (source >= 0) & (source < n)

            @pl.when(there)
            def _():
                arrival(item, step, hops).wait_recv()

            @pl.when(there & has[step])
            def _():
                relay(item, step, hops).start()

    begin(0)
    for h in range(kv):
        q_in[h].wait()
        begin(1 + h)

    for h in range(kv):
        v_in[h].wait()
        vt_buf[h] = v_buf[h].astype(jnp.float32).T.astype(jnp.bfloat16)

    for hops in range(1, n):
        turn(0, hops)
        for h in range(kv):
            turn(1 + h, hops)

    length = meta[me, pl.ds(rows, 1), :]
    offset = jnp.zeros((1, 128), jnp.int32)
    for s in range(n):
        offset = offset + jnp.where(s < me, meta[s, pl.ds(rows, 1), :], 0)
    lane_row = lax.broadcasted_iota(jnp.int32, (1, lanes), 1) // group
    slot_ids = lax.broadcasted_iota(jnp.int32, (KB, lanes), 0)

    def part(h, dest):
        pieces = []
        limit = jnp.zeros((1, lanes), jnp.int32)
        for r in range(rows):
            row = order_ref[0, dest * rows + r]
            pieces.append(q_all[h, row])
            limit = jnp.where(lane_row == r, meta[row // rows, pl.ds(row % rows, 1), :], limit)
        query = jnp.concatenate(pieces, axis=0)
        limit = jnp.minimum(length, limit - offset)
        outs, tots, tops = [], [], []
        for b in range(cap // KB):
            scores = lax.dot_general(
                k_buf[h, pl.ds(b * KB, KB), :], query, (((1,), (1,)), ((), ())),
                preferred_element_type=jnp.float32,
            )
            scores = jnp.where(slot_ids < limit - b * KB, scores, MASKED)
            top = jnp.max(scores, axis=0, keepdims=True)
            weights = jnp.exp2((scores - jnp.maximum(top, FLOOR)) * scale)
            tots.append(jnp.sum(weights, axis=0, keepdims=True))
            tops.append(top)
            outs.append(
                jnp.dot(
                    vt_buf[h, :, pl.ds(b * KB, KB)], weights.astype(jnp.bfloat16),
                    preferred_element_type=jnp.float32,
                )
            )
        return merge(outs, tots, tops)

    def merge(outs, tots, tops):
        best = functools.reduce(jnp.maximum, tops)
        out = tot = 0.0
        for o, t, p in zip(outs, tots, tops):
            factor = jnp.exp2((p - best) * scale)
            out = out + o * factor
            tot = tot + t * factor
        return out, tot, best

    def parcel(h, k):
        return pltpu.make_async_remote_copy(
            src_ref=sent.at[h, k], dst_ref=came.at[h, k],
            send_sem=part_send.at[h, k], recv_sem=part_recv.at[h, k],
            device_id={"blk": flipped(me, k, bits)}, device_id_type=MESH,
        )

    own = []
    for h in range(kv):
        k_in[h].wait()
        for k in range(n - 1, -1, -1):
            out, tot, top = part(h, flipped(me, k, bits))
            if k == 0:
                own.append((out, tot, top))
            else:
                sent[h, k, pl.ds(0, width), :] = out
                sent[h, k, pl.ds(width, 1), :] = tot
                sent[h, k, pl.ds(width + 1, 1), :] = top
                parcel(h, k).start()

    for h in range(kv):
        outs, tots, tops = ([x] for x in own[h])
        for k in range(n - 1, 0, -1):
            parcel(h, k).wait_recv()
            outs.append(came[h, k, pl.ds(0, width), :])
            tots.append(came[h, k, pl.ds(width, 1), :])
            tops.append(came[h, k, pl.ds(width + 1, 1), :])
        out, tot, _ = merge(outs, tots, tops)
        out_ref[:, h] = (out / tot).T.astype(jnp.bfloat16).reshape(rows, group, width)

    for h in range(kv):
        for k in range(n - 1, 0, -1):
            parcel(h, k).wait_send()
    for item in range(1 + kv):
        for hops in range(n - 1):
            for step in (1, -1):
                source = me - step * hops

                @pl.when((source >= 0) & (source < n) & has[step])
                def _():
                    relay(item, step, hops).wait_send()


def per_device(n, queries, positions, row_order, lengths, cache_keys, cache_values):
    keys, values = cache_keys[0], cache_values[0]
    kv, cap, width = keys.shape
    rows = queries.shape[1]
    group = queries.shape[2] // kv
    scale = float(width) ** -0.5 * math.log2(math.e)
    lanes = rows * group
    smem = pl.BlockSpec(memory_space=pltpu.SMEM)
    hbm = pl.BlockSpec(memory_space=pl.ANY)
    out = pl.pallas_call(
        functools.partial(kernel, n, scale),
        out_shape=jax.ShapeDtypeStruct((rows, kv, group, width), jnp.bfloat16),
        in_specs=[smem, smem, smem, hbm, hbm, hbm],
        out_specs=pl.BlockSpec(memory_space=pltpu.VMEM),
        scratch_shapes=[
            pltpu.VMEM((n, 2 * rows, 128), jnp.int32),
            pltpu.VMEM((kv, n * rows, group, width), jnp.bfloat16),
            pltpu.VMEM((kv, cap, width), jnp.bfloat16),
            pltpu.VMEM((kv, cap, width), jnp.bfloat16),
            pltpu.VMEM((kv, width, cap), jnp.bfloat16),
            pltpu.VMEM((kv, n, width + 8, lanes), jnp.float32),
            pltpu.VMEM((kv, n, width + 8, lanes), jnp.float32),
            pltpu.SemaphoreType.DMA((3 * kv,)),
            pltpu.SemaphoreType.DMA((1 + kv, 2, n)),
            pltpu.SemaphoreType.DMA((1 + kv, 2, n)),
            pltpu.SemaphoreType.DMA((kv, n)),
            pltpu.SemaphoreType.DMA((kv, n)),
        ],
        compiler_params=pltpu.CompilerParams(collective_id=0, has_side_effects=True),
        name="attend",
    )(
        positions, row_order, lengths,
        queries.reshape(rows, kv, group, width), keys, values,
    )
    return out.reshape(queries.shape)


def solution(mesh):
    placed = (
        P(("groups", "beam"), "blk", "heads", None),
        P(("groups", "beam"), "blk"),
        P(("groups", "beam"), None),
        P(("groups", "blk")),
        P(("groups", "blk"), "heads", None, None),
        P(("groups", "blk"), "heads", None, None),
    )
    return jax.shard_map(
        functools.partial(per_device, mesh.shape["blk"]),
        mesh=mesh,
        in_specs=placed,
        out_specs=P(("groups", "beam"), "blk", "heads", None),
        check_vma=False,
    )
```

time: 70.7 us -> 29.4 us (0.42)
  Pallas kernels: 0 us -> 27.1 us
  blocking collectives: 23.7 us -> 0 us
  waiting for transfers between devices: 14 us -> 0 us
  starting transfers between devices: 10.8 us -> 0 us
  local copies, waits for them, and re-layouts: 9.41 us -> 1.47 us
  other arithmetic: 5.07 us -> 0 us
  matrix products: 3.86 us -> 0 us
  loops' own time: 1.9 us -> 0 us
  between operations: 1.49 us -> 0.66 us
    pallas_call x0 -> x1, Pallas kernels: none -> 27.1 us  [per_device(): pl.pallas_call(functools.partial(kernel, n, scale), out_shape=jax.ShapeDt...]
    all_to_all x3 -> x0, waiting for transfers between devices: 14 us -> none  [the longest x1 8 us: per_device(): lax.all_to_all(merged_out[None], 'blk', split_axis=1, concat_axis=0, tile...]
    all_gather x1 -> x0, blocking collectives: 13.8 us -> none  [per_device(): piece_queries = lax.all_gather(queries, 'blk', axis=1, tiled=True)]
    all_to_all x3 -> x0, starting transfers between devices: 10.8 us -> none  [the longest x1 3.78 us: per_device(): lax.all_to_all(merged_top[None], 'blk', split_axis=1, concat_axis=0, tile...]
    unnamed x1 -> x0, blocking collectives: 9.92 us -> none
    dot_general x8 -> x0, matrix products: 3.86 us -> none  [the longest x4 2.34 us: block_partial(): jnp.einsum('rkgj,kjd->rkgd', weights.astype(jnp.bfloat16), value_block, p...]
    unnamed x20 -> x1, local copies, waits for them, and re-layouts: 4.28 us -> 1.47 us
    convert_element_type x4 -> x0, other arithmetic: 1.92 us -> none  [the longest x3 1.18 us: block_partial(): weights.astype(jnp.bfloat16)]
  transfers between devices with their start and end apart: 3 -> 0, of which waited for: 3 -> 0; matrix products, arithmetic and copies ran while one was open for 10% -> 0% of each run, Pallas kernels for 0% -> 0%
where the time goes in v1:
time: 29.4 us; the launch traced here: 29.2 us
  Pallas kernels  27.1 us (92%)
  local copies, waits for them, and re-layouts  1.47 us (5%)
  between operations  0.66 us (2%)
    pallas_call x1, Pallas kernels, per_device(): pl.pallas_call(functools.partial(kernel, n, scale), out_shape=jax.ShapeDt...  27.1 us
    unnamed x1, local copies, waits for them, and re-layouts  1.47 us

profile of v1, /device:TPU:0, one launch (start us, length us, event | category | flops | bytes accessed | tf_op | source)
XLA Modules:
  0.0 29.2 jit_solution(18082346137782640520)
XLA Ops:
  0.7 27.1 %attend.1 = bf16[8,2,16,128]{3,2,1,0:T(8,128)(2,1)} custom-call(s32[1,8]{1,0:T(1,128)} %pos_ref.1, s32[1,32]{1,0:T(1,128)} %order_ref.1, s32[1]{0:T(128)S(6)} %copy.8.len_ref, bf16[8,2,16,128]{3,2,1,0:T(8,128)(2,1)} %bitcast.7, bf16[2,1024,128]{2,1,0:T(8,128)(2,1)} %bitcast.4, bf16[2,1024,128]{2,1,0:T(8,128)(2,1)} %bitcast.5), custom_call_target="tpu_custom_call" | custom-call | tf_op jit(solution)/shard_map/attend/pallas_call | solution.py:215
  27.8 1.5 %copy.9 = bf16[1,8,32,128]{3,2,1,0:T(8,128)(2,1)} copy(bf16[1,8,32,128]{3,2,1,0:T(8,128)(2,1)} %bitcast.6) | data formatting | bytes 131072

commit v2 on v1

--- a/solution.py
+++ b/solution.py
@@ -37,7 +37,7 @@
 
     q_in = [
         pltpu.make_async_copy(
-            q_hbm.at[:, h], q_all.at[h, pl.ds(me * rows, rows)], local_sem.at[2 * kv + h]
+            q_hbm.at[:, h], q_all[h].at[pl.ds(me * rows, rows)], local_sem.at[2 * kv + h]
         )
         for h in range(kv)
     ]
@@ -52,16 +52,17 @@
 
     barrier = pltpu.get_barrier_semaphore()
     has = {1: me + 1 < n, -1: me >= 1}
-    for k in range(1, n):
-        pl.semaphore_signal(
-            barrier, inc=1, device_id={"blk": flipped(me, k, bits)}, device_id_type=MESH
-        )
-    pl.semaphore_wait(barrier, n - 1)
+    for step in (1, -1):
+        @pl.when(has[step])
+        def _():
+            pl.semaphore_signal(barrier, inc=1, device_id={"blk": me + step}, device_id_type=MESH)
+
+    pl.semaphore_wait(barrier, has[1].astype(jnp.int32) + has[-1].astype(jnp.int32))
 
     def slot(item, source):
         if item == 0:
             return meta.at[source]
-        return q_all.at[item - 1, pl.ds(source * rows, rows)]
+        return q_all[item - 1].at[pl.ds(source * rows, rows)]
 
     def relay(item, step, hops):
         way = 0 if step == 1 else 1
@@ -113,8 +114,10 @@
 
     for hops in range(1, n):
         turn(0, hops)
-        for h in range(kv):
-            turn(1 + h, hops)
+        turn(1, hops)
+        if hops == 1:
+            for h in range(1, kv):
+                turn(1 + h, hops)
 
     length = meta[me, pl.ds(rows, 1), :]
     offset = jnp.zeros((1, 128), jnp.int32)
@@ -128,7 +131,7 @@
         limit = jnp.zeros((1, lanes), jnp.int32)
         for r in range(rows):
             row = order_ref[0, dest * rows + r]
-            pieces.append(q_all[h, row])
+            pieces.append(q_all[h][row])
             limit = jnp.where(lane_row == r, meta[row // rows, pl.ds(row % rows, 1), :], limit)
         query = jnp.concatenate(pieces, axis=0)
         limit = jnp.minimum(length, limit - offset)
@@ -179,6 +182,8 @@
                 sent[h, k, pl.ds(width, 1), :] = tot
                 sent[h, k, pl.ds(width + 1, 1), :] = top
                 parcel(h, k).start()
+            if h + 1 < kv and 2 <= n - k + 1 < n:
+                turn(2 + h, n - k + 1)
 
     for h in range(kv):
         outs, tots, tops = ([x] for x in own[h])
@@ -219,7 +224,7 @@
         out_specs=pl.BlockSpec(memory_space=pltpu.VMEM),
         scratch_shapes=[
             pltpu.VMEM((n, 2 * rows, 128), jnp.int32),
-            pltpu.VMEM((kv, n * rows, group, width), jnp.bfloat16),
+            [pltpu.VMEM((n * rows, group, width), jnp.bfloat16) for _ in range(kv)],
             pltpu.VMEM((kv, cap, width), jnp.bfloat16),
             pltpu.VMEM((kv, cap, width), jnp.bfloat16),
             pltpu.VMEM((kv, width, cap), jnp.bfloat16),

time: 29.4 us -> 27.8 us (0.946)
  Pallas kernels: 27.1 us -> 25.5 us
    pallas_call x1, Pallas kernels: 27.1 us -> 25.5 us  [per_device(): pl.pallas_call(functools.partial(kernel, n, scale), out_shape=jax.ShapeDt...]
where the time goes in v2:
time: 27.8 us; the launch traced here: 27.6 us
  Pallas kernels  25.5 us (92%)
  local copies, waits for them, and re-layouts  1.47 us (5%)
  between operations  0.66 us (2%)
    pallas_call x1, Pallas kernels, per_device(): pl.pallas_call(functools.partial(kernel, n, scale), out_shape=jax.ShapeDt...  25.5 us
    unnamed x1, local copies, waits for them, and re-layouts  1.47 us

profile of v2, /device:TPU:0, one launch (start us, length us, event | category | flops | bytes accessed | tf_op | source)
XLA Modules:
  0.0 27.6 jit_solution(15945232844951466681)
XLA Ops:
  0.7 25.5 %attend.1 = bf16[8,2,16,128]{3,2,1,0:T(8,128)(2,1)} custom-call(s32[1,8]{1,0:T(1,128)} %pos_ref.1, s32[1,32]{1,0:T(1,128)} %order_ref.1, s32[1]{0:T(128)S(6)} %copy.8.len_ref, bf16[8,2,16,128]{3,2,1,0:T(8,128)(2,1)} %bitcast.7, bf16[2,1024,128]{2,1,0:T(8,128)(2,1)} %bitcast.4, bf16[2,1024,128]{2,1,0:T(8,128)(2,1)} %bitcast.5), custom_call_target="tpu_custom_call" | custom-call | tf_op jit(solution)/shard_map/attend/pallas_call | solution.py:220
  26.2 1.5 %copy.9 = bf16[1,8,32,128]{3,2,1,0:T(8,128)(2,1)} copy(bf16[1,8,32,128]{3,2,1,0:T(8,128)(2,1)} %bitcast.6) | data formatting | bytes 131072
